TPU v7x, 32 devices: a whole 2x2x4 slice. The times are simulated.
32 devices in a mesh: dp: 8 (over y, x, core), tensor: 4 (over z).
Axes of the slice: x: 2, y: 2, z: 4, core: 2. Of those that a mesh axis runs over, the one named last changes fastest.
Arguments:
- tokens: bfloat16 [8192, 1024], P(('dp', 'tensor')), may hold values from -6 to 6
- upstream: bfloat16 [8192, 1024], P(('dp', 'tensor')), may hold values from -6 to 6
- counts: int32 [128], P('dp'), may hold values from 37 to 49, as said below
- norm_gain: float32 [1024], replicated, may hold values from 0.5 to 1.5
- norm_bias: float32 [1024], replicated, may hold values from -4 to 4
- w_qkv: bfloat16 [1024, 3072], P('dp', 'tensor'), may hold values from -0.1875 to 0.1875
- w_out: bfloat16 [1024, 1024], P('tensor', 'dp'), may hold values from -0.1875 to 0.1875
Outputs:
- grad_tokens: bfloat16 [8192, 1024], P(('dp', 'tensor'))
- grad_qkv: float32 [1024, 3072], P('dp', 'tensor')
- grad_out: float32 [1024, 1024], P('tensor', 'dp')
- grad_gain: float32 [1024], replicated
- grad_bias: float32 [1024], replicated
Inputs may be any that keep to these rules, and one draw needn't show every extreme that they name: counts[i] is the number of visible tokens of image i, held in its first slots; some image has 49 in every draw.
All inputs are finite; a program needn't handle non-finite values.
Results may differ from a plain program's by a relative error of at most 0.014.
Values may be sent and summed in bfloat16 or wider, within the bound.
A program may use at most 64 MiB of HBM per device.

v0:
```python
import jax
import jax.numpy as jnp
from jax import lax
from jax.sharding import PartitionSpec as P

HEAD = 64
CAP = 64


def layer_norm(tokens, norm_gain, norm_bias):
    values = tokens.astype(jnp.float32)
    centre = jnp.mean(values, axis=-1, keepdims=True)
    shifted = values - centre
    variance = jnp.mean(shifted * shifted, axis=-1, keepdims=True)
    inverse_std = lax.rsqrt(variance + 1e-06)
    scaled = shifted * inverse_std
    normed = (scaled * norm_gain + norm_bias).astype(jnp.bfloat16)
    return (normed, scaled, inverse_std)


def on_device(tokens, upstream, counts, norm_gain, norm_bias, w_qkv, w_out):
    local_rows = tokens.shape[0]
    own_images = local_rows // CAP
    start_image = lax.axis_index("tensor") * own_images
    own_counts = lax.dynamic_slice_in_dim(counts, start_image, own_images)
    own_live = (
        (jnp.arange(CAP, dtype=jnp.int32)[None, :] < own_counts[:, None])
        .reshape(-1)
        .astype(jnp.float32)
    )
    normed, scaled, inverse_std = layer_norm(tokens, norm_gain, norm_bias)
    all_normed = lax.all_gather(normed, "tensor", axis=0, tiled=True)
    qkv_cols = lax.all_gather(w_qkv, "dp", axis=0, tiled=True)
    out_rows = lax.all_gather(w_out, "dp", axis=1, tiled=True)
    all_upstream = lax.all_gather(upstream, "tensor", axis=0, tiled=True)
    group_rows = all_normed.shape[0]
    images = group_rows // CAP
    local_heads = qkv_cols.shape[1] // (3 * HEAD)
    slot_live = jnp.arange(CAP, dtype=jnp.int32)[None, :] < counts[:, None]
    group_live = slot_live.reshape(-1).astype(jnp.bfloat16)
    masked = all_upstream * group_live[:, None]
    projected = jnp.dot(all_normed, qkv_cols, preferred_element_type=jnp.float32).astype(
        jnp.bfloat16
    )
    projected = projected.reshape(images, CAP, local_heads, 3, HEAD)
    query_rows = projected[:, :, :, 0]
    key_rows = projected[:, :, :, 1]
    value_rows = projected[:, :, :, 2]
    score_scale = 1.0 / HEAD**0.5
    scores = (
        jnp.einsum("bqhe,bkhe->bhqk", query_rows, key_rows, preferred_element_type=jnp.float32)
        * score_scale
    )
    scores = jnp.where(slot_live[:, None, None, :], scores, -1e30)
    probs = jax.nn.softmax(scores, axis=-1)
    probs_low = probs.astype(jnp.bfloat16)
    attended = jnp.einsum(
        "bhqk,bkhe->bqhe", probs_low, value_rows, preferred_element_type=jnp.float32
    )
    attended = attended.astype(jnp.bfloat16).reshape(group_rows, local_heads * HEAD)
    out_part = lax.dot_general(
        attended, masked, (((0,), (0,)), ((), ())), preferred_element_type=jnp.float32
    )
    grad_out = lax.psum_scatter(
        out_part.astype(jnp.bfloat16), "dp", scatter_dimension=1, tiled=True
    ).astype(jnp.float32)
    grad_att = lax.dot_general(
        masked, out_rows, (((1,), (1,)), ((), ())), preferred_element_type=jnp.float32
    )
    grad_att = grad_att.astype(jnp.bfloat16).reshape(images, CAP, local_heads, HEAD)
    grad_probs = jnp.einsum(
        "bqhe,bkhe->bhqk", grad_att, value_rows, preferred_element_type=jnp.float32
    )
    row_delta = jnp.sum(probs * grad_probs, axis=-1, keepdims=True)
    grad_scores = (probs * (grad_probs - row_delta) * score_scale).astype(jnp.bfloat16)
    grad_value = jnp.einsum(
        "bhqk,bqhe->bkhe", probs_low, grad_att, preferred_element_type=jnp.float32
    ).astype(jnp.bfloat16)
    grad_query = jnp.einsum(
        "bhqk,bkhe->bqhe", grad_scores, key_rows, preferred_element_type=jnp.float32
    ).astype(jnp.bfloat16)
    grad_key = jnp.einsum(
        "bhqk,bqhe->bkhe", grad_scores, query_rows, preferred_element_type=jnp.float32
    ).astype(jnp.bfloat16)
    grad_proj = jnp.stack([grad_query, grad_key, grad_value], axis=3).reshape(
        group_rows, 3 * local_heads * HEAD
    )
    qkv_part = lax.dot_general(
        all_normed, grad_proj, (((0,), (0,)), ((), ())), preferred_element_type=jnp.float32
    )
    grad_qkv = lax.psum_scatter(
        qkv_part.astype(jnp.bfloat16), "dp", scatter_dimension=0, tiled=True
    ).astype(jnp.float32)
    grad_normed = lax.psum_scatter(
        lax.dot_general(
            grad_proj, qkv_cols, (((1,), (1,)), ((), ())), preferred_element_type=jnp.float32
        ).astype(jnp.bfloat16),
        "tensor",
        scatter_dimension=0,
        tiled=True,
    ).astype(jnp.float32)
    grad_gain, grad_bias = lax.psum(
        (jnp.sum(grad_normed * scaled, axis=0), jnp.sum(grad_normed, axis=0)), ("dp", "tensor")
    )
    grad_scaled = grad_normed * norm_gain
    grad_ln = inverse_std * (
        grad_scaled
        - jnp.mean(grad_scaled, axis=-1, keepdims=True)
        - scaled * jnp.mean(grad_scaled * scaled, axis=-1, keepdims=True)
    )
    grad_tokens = (upstream.astype(jnp.float32) * own_live[:, None] + grad_ln).astype(jnp.bfloat16)
    return (grad_tokens, grad_qkv, grad_out, grad_gain, grad_bias)


def solution(mesh):
    return jax.shard_map(
        on_device,
        mesh=mesh,
        in_specs=(
            P(("dp", "tensor"), None),
            P(("dp", "tensor"), None),
            P("dp"),
            P(),
            P(),
            P("dp", "tensor"),
            P("tensor", "dp"),
        ),
        out_specs=(P(("dp", "tensor"), None), P("dp", "tensor"), P("tensor", "dp"), P(), P()),
        check_vma=False,
    )
```

profile of v0, /device:TPU:0, one launch (start us, length us, event | category | flops | bytes accessed | tf_op | source)
XLA Modules:
  0.0 332.8 jit_solution(4929097271266516613)
XLA Ops:
  13.6 12.6 %all_gather.15 = bf16[256,1024]{1,0:T(8,128)(2,1)S(1)} all-gather(bf16[256,128]{1,0:T(8,128)(2,1)S(1)} %copy-done.6), channel_id=1, replica_groups=mesh['dp'=8,'tensor'=4] {'dp'}, dimensions={1}, use_global_device_ids=true | all-gather | bytes 589824 | tf_op jit(solution)/shard_map/all_gather | solution.py:34
  26.2 12.7 %all-gather.6.cloned.1.call-done = bf16[1024,768]{1,0:T(8,128)(2,1)} async-done(((bf16[128,768]{1,0:T(8,128)(2,1)}), bf16[1024,768]{1,0:T(8,128)(2,1)}) %all-gather.6.cloned.1.call-update) | async-done | bytes 1572880 | tf_op jit(solution)/shard_map/all_gather | solution.py:33
  38.9 47.8 %all-gather.4.cloned.1.call-done = bf16[1024,1024]{1,0:T(8,128)(2,1)} async-done(((bf16[256,1024]{1,0:T(8,128)(2,1)}), bf16[1024,1024]{1,0:T(8,128)(2,1)}) %all-gather.4.cloned.1.call-update) | async-done | bytes 2097168 | tf_op jit(solution)/shard_map/all_gather | solution.py:32
  86.7 3.8 %convolution_convert_fusion.2 = bf16[1024,768]{1,0:T(8,128)(2,1)S(1)} fusion(bf16[1024,1024]{1,0:T(8,128)(2,1)} %all-gather.4.cloned.1.call-done, bf16[1024,768]{1,0:T(8,128)(2,1)} %all-gather.6.cloned.1.call-done), kind=kOutput, calls=%fused_computation.15 | convolution fusion | flops 1611399168 | bytes 5242880 | tf_op jit(solution)/shard_map/dot_general | solution.py:42
  90.6 5.0 %reshape.105 = bf16[16,64,4,3,64]{4,3,2,1,0:T(4,128)(2,1)} reshape(bf16[1024,768]{1,0:T(8,128)(2,1)S(1)} %convolution_convert_fusion.2) | data formatting | bytes 3145728 | tf_op jit(solution)/shard_map/reshape | solution.py:45
  95.5 11.4 %fusion.71 = (bf16[16,64,4,1,64]{4,3,2,1,0:T(2,128)(2,1)S(1)}, bf16[16,64,4,1,64]{4,3,2,1,0:T(2,128)(2,1)}, bf16[16,64,4,1,64]{4,3,2,1,0:T(2,128)(2,1)}) fusion(bf16[16,64,4,3,64]{4,3,2,1,0:T(4,128)(2,1)} %reshape.105), kind=kLoop, calls=%fused_computation.78 | loop fusion | bytes 3145728 | tf_op jit(solution)/shard_map/slice | solution.py:48
  106.9 25.9 %all-gather.8.cloned.1.call-done = bf16[1024,1024]{1,0:T(8,128)(2,1)} async-done(((bf16[256,1024]{1,0:T(8,128)(2,1)}), bf16[1024,1024]{1,0:T(8,128)(2,1)}) %all-gather.8.cloned.1.call-update) | async-done | bytes 2097168 | tf_op jit(solution)/shard_map/all_gather | solution.py:35
  132.8 3.1 fusion.33
  139.3 2.9 fusion.62
  142.3 4.8 %fusion.72 = (f32[16,4,64]{2,1,0:T(4,128)S(1)}, f32[16,4,64,64]{2,3,1,0:T(8,128)}) fusion(pred[16,64]{1,0:T(8,128)(4,1)S(1)} %get-tuple-element.14, bf16[16,64,4,1,64]{4,3,2,1,0:T(2,128)(2,1)} %get-tuple-element.13, bf16[16,64,4,1,64]{4,3,2,1,0:T(2,128)(2,1)} %get-tuple-element.12), kind=kOutput, calls=%fused_computation.79 | convolution fusion | flops 34603072 | bytes 2114560 | tf_op jit(solution)/shard_map/sub | solution.py:55
  147.1 3.4 %fusion.25 = bf16[16,64,4,1,64]{1,4,2,0,3:T(8,128)(2,1)} fusion(bf16[16,64,4,64]{1,3,2,0:T(8,128)(2,1)S(1)} %copy-done.1, f32[16,4,64,64]{2,3,1,0:T(8,128)} %get-tuple-element.17, f32[16,4,64]{2,1,0:T(4,128)S(1)} %get-tuple-element.16), kind=kOutput, calls=%fused_computation.28 | convolution fusion | flops 34340864 | bytes 2113536 | tf_op jit(solution)/shard_map/bhqk,bqhe->bkhe/dot_general | solution.py:76
  151.0 6.1 %fusion.30 = bf16[16,64,4,1,64]{1,4,2,0,3:T(8,128)(2,1)} fusion(f32[16,4,64,64]{2,3,1,0:T(8,128)} %fusion.62, bf16[16,64,4,1,64]{4,3,2,1,0:T(2,128)(2,1)} %get-tuple-element.13, f32[16,4,64,64]{2,3,1,0:T(8,128)} %get-tuple-element.17, f32[16,4,64]{2,1,0:T(4,128)S(1)} %get-tuple-element.16), kind=kOutput, calls=%fused_computation.31 | convolution fusion | flops 35655744 | bytes 3162112 | tf_op jit(solution)/shard_map/bhqk,bkhe->bqhe/dot_general | solution.py:79
  158.5 2.5 fusion.36
  162.3 5.6 %fusion.27 = bf16[16,64,4,1,64]{1,4,2,0,3:T(8,128)(2,1)} fusion(f32[16,4,64,64]{2,3,1,0:T(8,128)} %fusion.62, bf16[16,64,4,1,64]{4,3,2,1,0:T(2,128)(2,1)S(1)} %copy-done.3, f32[16,4,64,64]{2,3,1,0:T(8,128)} %get-tuple-element.17, f32[16,4,64]{2,1,0:T(4,128)S(1)} %get-tuple-element.16), kind=kOutput, calls=%fused_computation.30 | convolution fusion | flops 35655744 | bytes 3162112 | tf_op jit(solution)/shard_map/bhqk,bqhe->bkhe/dot_general | solution.py:82
  167.9 2.3 pad_maximum_fusion
  170.2 2.4 copy.50
  172.7 3.2 reshape.99
  175.9 5.2 %convolution_convert_fusion.1 = bf16[1024,768]{1,0:T(8,128)(2,1)} fusion(bf16[1024,1024]{1,0:T(8,128)(2,1)} %all-gather.4.cloned.1.call-done, bf16[1024,768]{0,1:T(8,128)(2,1)} %reshape.99), kind=kOutput, calls=%fused_computation.14 | convolution fusion | flops 1611399168 | bytes 5242880 | tf_op jit(solution)/shard_map/dot_general | solution.py:88
  181.2 3.2 convolution_convert_fusion
  184.6 10.5 %reduce-scatter.10.cloned.1.call-done = bf16[128,256]{1,0:T(8,128)(2,1)} async-done(((bf16[1024,256]{1,0:T(8,128)(2,1)}), bf16[128,256]{1,0:T(8,128)(2,1)}) %reduce-scatter.10.cloned.1.call-update) | async-done | bytes 65552
  196.8 39.9 %reduce-scatter.8.cloned.1.call-done = bf16[128,768]{1,0:T(8,128)(2,1)} async-done(((bf16[1024,768]{1,0:T(8,128)(2,1)}), bf16[128,768]{1,0:T(8,128)(2,1)}) %reduce-scatter.8.cloned.1.call-update) | async-done | bytes 196624 | tf_op jit(solution)/shard_map/reduce_scatter | solution.py:91
  238.4 44.1 %reduce-scatter.6.cloned.1.call-done = bf16[256,1024]{1,0:T(8,128)(2,1)} async-done(((bf16[1024,1024]{1,0:T(8,128)(2,1)}), bf16[256,1024]{1,0:T(8,128)(2,1)}) %reduce-scatter.6.cloned.1.call-update) | async-done | bytes 524304 | tf_op jit(solution)/shard_map/reduce_scatter | solution.py:94
  284.1 39.5 %all-reduce = (f32[1024]{0:T(1024)}, f32[1024]{0:T(1024)}) all-reduce(f32[1024]{0:T(1024)S(1)} %get-tuple-element.5, f32[1024]{0:T(1024)S(1)} %get-tuple-element.8), channel_id=1, replica_groups=mesh['dp'=8,'tensor'=4] {'dp','tensor'}, use_global_device_ids=true, to_apply=%region_11.12 | all-reduce | flops 2048 | bytes 16384 | tf_op jit(solution)/shard_map/psum | solution.py:102
  323.6 2.3 fusion.48
  (55 shorter events, 18.2 us)
Async XLA Ops:
  7.2 6.3 %copy-start.8 = (s32[16]{0:T(128)S(1)}, s32[16]{0:T(128)}, u32[]{:S(2)}) copy-start(s32[16]{0:T(128)} %param.9) | copy-start | bytes 196
  7.2 6.4 %copy-start.6 = (bf16[256,128]{1,0:T(8,128)(2,1)S(1)}, bf16[256,128]{1,0:T(8,128)(2,1)}, u32[]{:S(2)}) copy-start(bf16[256,128]{1,0:T(8,128)(2,1)} %param.13) | copy-start | bytes 196612
  7.2 31.7 %all-gather.6.cloned.1.call-start = ((), (), s32[]{:S(2)}) async-start(), calls=%async_computation.4 | async-start | bytes 1769472 | tf_op jit(solution)/shard_map/all_gather | solution.py:33
  7.9 78.8 %all-gather.4.cloned.1.call-start = ((), (), s32[]{:S(2)}) async-start(), calls=%async_computation.3 | async-start | bytes 2621440 | tf_op jit(solution)/shard_map/all_gather | solution.py:32
  12.7 120.2 %all-gather.8.cloned.1.call-start = ((), (), s32[]{:S(2)}) async-start(), calls=%async_computation.5 | async-start | bytes 2621440 | tf_op jit(solution)/shard_map/all_gather | solution.py:35
  13.4 181.8 %reduce-scatter.10.cloned.1.call-start = ((), (), s32[]{:S(2)}) async-start(), calls=%async_computation.8 | async-start | bytes 589824
  142.3 4.8 %copy-start.1 = (bf16[16,64,4,64]{1,3,2,0:T(8,128)(2,1)S(1)}, bf16[16,64,4,64]{1,3,2,0:T(8,128)(2,1)}, u32[]{:S(2)}) copy-start(bf16[16,64,4,64]{1,3,2,0:T(8,128)(2,1)} %copy.48) | copy-start | bytes 1572868
  147.1 3.4 %copy-start.10 = (f32[16,4,64,64]{2,3,1,0:T(8,128)S(1)}, f32[16,4,64,64]{2,3,1,0:T(8,128)}, u32[]{:S(2)}) copy-start(f32[16,4,64,64]{2,3,1,0:T(8,128)} %get-tuple-element.17) | copy-start | bytes 3145732
  158.5 3.8 %copy-start.3 = (bf16[16,64,4,1,64]{4,3,2,1,0:T(2,128)(2,1)S(1)}, bf16[16,64,4,1,64]{4,3,2,1,0:T(2,128)(2,1)}, u32[]{:S(2)}) copy-start(bf16[16,64,4,1,64]{4,3,2,1,0:T(2,128)(2,1)} %get-tuple-element.12) | copy-start | bytes 1572868
  162.1 5.8 %copy-start.5 = (bf16[16,64,4,1,64]{1,4,2,0,3:T(8,128)(2,1)S(1)}, bf16[16,64,4,1,64]{1,4,2,0,3:T(8,128)(2,1)}, u32[]{:S(2)}) copy-start(bf16[16,64,4,1,64]{1,4,2,0,3:T(8,128)(2,1)} %fusion.25) | copy-start | bytes 1572868
  162.1 74.6 %reduce-scatter.8.cloned.1.call-start = ((), (), s32[]{:S(2)}) async-start(), calls=%async_computation.7 | async-start | bytes 1769472 | tf_op jit(solution)/shard_map/reduce_scatter | solution.py:91
  175.9 5.3 %copy-start.4 = (bf16[1024,768]{0,1:T(8,128)(2,1)S(1)}, bf16[1024,768]{0,1:T(8,128)(2,1)}, u32[]{:S(2)}) copy-start(bf16[1024,768]{0,1:T(8,128)(2,1)} %reshape.99) | copy-start | bytes 4718596
  175.9 5.3 %copy-start.9 = (bf16[1024,768]{1,0:T(8,128)(2,1)S(1)}, bf16[1024,768]{1,0:T(8,128)(2,1)}, u32[]{:S(2)}) copy-start(bf16[1024,768]{1,0:T(8,128)(2,1)} %all-gather.6.cloned.1.call-done) | copy-start | bytes 4718596
  181.1 101.4 %reduce-scatter.6.cloned.1.call-start = ((), (), s32[]{:S(2)}) async-start(), calls=%async_computation.6 | async-start | bytes 2621440 | tf_op jit(solution)/shard_map/reduce_scatter | solution.py:94
  184.3 98.2 %copy-start = (bf16[256,1024]{1,0:T(8,128)(2,1)S(1)}, bf16[256,1024]{1,0:T(8,128)(2,1)}, u32[]{:S(2)}) copy-start(bf16[256,1024]{1,0:T(8,128)(2,1)} %param.7) | copy-start | bytes 1572868
  184.4 98.2 %copy-start.7 = (f32[1024]{0:T(1024)S(1)}, f32[1024]{0:T(1024)}, u32[]{:S(2)}) copy-start(f32[1024]{0:T(1024)} %param.10) | copy-start | bytes 12292
  184.4 139.3 %copy-start.2 = (bf16[256,1024]{1,0:T(8,128)(2,1)S(1)}, bf16[256,1024]{1,0:T(8,128)(2,1)}, u32[]{:S(2)}) copy-start(bf16[256,1024]{1,0:T(8,128)(2,1)} %param.8) | copy-start | bytes 1572868
Sparse Core Ops, SparseCore 0:
  9.9 28.9 all-gather.5
  41.0 45.6 all-gather.3
  88.3 44.4 all-gather.7
  162.2 32.9 reduce-scatter.9
  198.3 38.3 reduce-scatter.7
  238.8 43.6 reduce-scatter.5
where the time goes:
time: 333 us
  waiting for transfers between devices  182 us (55%)
  blocking collectives  52.1 us (16%)
  matrix products  41.2 us (12%)
  local copies, waits for them, and re-layouts  29 us (9%)
  between operations  14.3 us (4%)
  other arithmetic  13.4 us (4%)
    all_gather x1, waiting for transfers between devices, on_device(): all_normed = lax.all_gather(normed, 'tensor', axis=0, tiled=True)  47.8 us
    reduce_scatter x1, waiting for transfers between devices, on_device(): lax.psum_scatter(lax.dot_general(grad_proj, qkv_cols, (((1,), (1,)), ((),...  44.1 us
    reduce_scatter x1, waiting for transfers between devices, on_device(): lax.psum_scatter(qkv_part.astype(jnp.bfloat16), 'dp', scatter_dimension=0...  39.9 us
    psum x1, blocking collectives, on_device(): lax.psum((jnp.sum(grad_normed * scaled, axis=0), jnp.sum(grad_normed, axi...  39.5 us
    all_gather x1, waiting for transfers between devices, on_device(): all_upstream = lax.all_gather(upstream, 'tensor', axis=0, tiled=True)  25.9 us
    all_gather x1, waiting for transfers between devices, on_device(): qkv_cols = lax.all_gather(w_qkv, 'dp', axis=0, tiled=True)  12.7 us
    all_gather x1, blocking collectives, on_device(): out_rows = lax.all_gather(w_out, 'dp', axis=1, tiled=True)  12.6 us
    unnamed x7, waiting for transfers between devices  12 us
  transfers between devices with their start and end apart: 6, of which 6 were waited for; matrix products, arithmetic and copies ran while one was open for 15% of the time, Pallas kernels for 0%

commit v1 on v0

--- a/solution.py
+++ b/solution.py
@@ -29,7 +29,14 @@
         .astype(jnp.float32)
     )
     normed, scaled, inverse_std = layer_norm(tokens, norm_gain, norm_bias)
-    all_normed = lax.all_gather(normed, "tensor", axis=0, tiled=True)
+    ring = [normed]
+    for hop in range(3):
+        ring.append(lax.ppermute(ring[-1], "tensor", [(dev, (dev + 1) % 4) for dev in range(4)]))
+    all_normed = jnp.roll(
+        jnp.concatenate(ring[::-1], axis=0),
+        (lax.axis_index("tensor") + 1) * ring[0].shape[0],
+        axis=0,
+    )
     qkv_cols = lax.all_gather(w_qkv, "dp", axis=0, tiled=True)
     out_rows = lax.all_gather(w_out, "dp", axis=1, tiled=True)
     all_upstream = lax.all_gather(upstream, "tensor", axis=0, tiled=True)

time: 333 us -> 290 us (0.87)
  waiting for transfers between devices: 182 us -> 122 us
  local copies, waits for them, and re-layouts: 29 us -> 42.2 us
    all_gather x1 -> x0, waiting for transfers between devices: 47.8 us -> none  [on_device(): all_normed = lax.all_gather(normed, 'tensor', axis=0, tiled=True)]
    ppermute x0 -> x3, waiting for transfers between devices: none -> 32.5 us  [on_device(): lax.ppermute(ring[-1], 'tensor', [(dev, (dev + 1) % 4) for dev in range(4)])]
    all_gather x1, waiting for transfers between devices: 25.9 us -> 0.02 us  [on_device(): all_upstream = lax.all_gather(upstream, 'tensor', axis=0, tiled=True)]
    all_gather x1, waiting for transfers between devices: 12.7 us -> 0.01 us  [on_device(): qkv_cols = lax.all_gather(w_qkv, 'dp', axis=0, tiled=True)]
    unnamed x7 -> x6, waiting for transfers between devices: 12 us -> 5.52 us
    unnamed x24 -> x28, local copies, waits for them, and re-layouts: 1.99 us -> 8.12 us
  transfers between devices with their start and end apart: 6 -> 8, of which waited for: 6 -> 6; matrix products, arithmetic and copies ran while one was open for 15% -> 25% of each run, Pallas kernels for 0% -> 0%
where the time goes in v1:
time: 290 us; the launch traced here: 289 us
  waiting for transfers between devices  122 us (42%)
  blocking collectives  50.3 us (17%)
  local copies, waits for them, and re-layouts  42.2 us (15%)
  matrix products  42.2 us (15%)
  other arithmetic  15.1 us (5%)
  between operations  13.9 us (5%)
  starting transfers between devices  3.53 us (1%)
    reduce_scatter x1, waiting for transfers between devices, on_device(): lax.psum_scatter(lax.dot_general(grad_proj, qkv_cols, (((1,), (1,)), ((),...  44.1 us
    reduce_scatter x1, waiting for transfers between devices, on_device(): lax.psum_scatter(qkv_part.astype(jnp.bfloat16), 'dp', scatter_dimension=0...  39.9 us
    psum x1, blocking collectives, on_device(): lax.psum((jnp.sum(grad_normed * scaled, axis=0), jnp.sum(grad_normed, axi...  39.5 us
    ppermute x3, waiting for transfers between devices, on_device(): lax.ppermute(ring[-1], 'tensor', [(dev, (dev + 1) % 4) for dev in range(4)])  32.5 us
    slice x1, local copies, waits for them, and re-layouts, on_device(): value_rows = projected[:, :, :, 2]  11.3 us
    all_gather x1, blocking collectives, on_device(): out_rows = lax.all_gather(w_out, 'dp', axis=1, tiled=True)  10.8 us
    unnamed x28, local copies, waits for them, and re-layouts  8.12 us
  transfers between devices with their start and end apart: 8, of which 6 were waited for; matrix products, arithmetic and copies ran while one was open for 25% of the time, Pallas kernels for 0%

profile of v1, /device:TPU:0, one launch (start us, length us, event | category | flops | bytes accessed | tf_op | source)
XLA Modules:
  0.0 289.4 jit_solution(14829815670892496258)
XLA Ops:
  11.9 3.1 %collective-permute-start = (bf16[256,1024]{1,0:T(8,128)(2,1)S(1)}, bf16[256,1024]{1,0:T(8,128)(2,1)S(1)}, u32[]{:S(2)}, u32[]{:S(2)}) collective-permute-start(bf16[256,1024]{1,0:T(8,128)(2,1)S(1)} %fusion.54), channel_id=1, source_target_pairs={{0,1},{1,2},{2,3},{3,0},{4,5},{5,6},{6,7},{7,4},{8,9},{9,10},{10,1... | collective-permute-start | bytes 1572872 | tf_op jit(solution)/shard_map/ppermute | solution.py:34
  15.0 13.9 %collective-permute-done = bf16[256,1024]{1,0:T(8,128)(2,1)S(1)} collective-permute-done((bf16[256,1024]{1,0:T(8,128)(2,1)S(1)}, bf16[256,1024]{1,0:T(8,128)(2,1)S(1)}, u32[]{:S(2)}, u32[]{:S(2)}) %collective-permute-start) | collective-permute-done | bytes 524320 | tf_op jit(solution)/shard_map/ppermute | solution.py:34
  28.9 14.9 %collective-permute-done.1 = bf16[256,1024]{1,0:T(8,128)(2,1)S(1)} collective-permute-done((bf16[256,1024]{1,0:T(8,128)(2,1)S(1)}, bf16[256,1024]{1,0:T(8,128)(2,1)S(1)}, u32[]{:S(2)}, u32[]{:S(2)}) %collective-permute-start.1) | collective-permute-done | bytes 524320 | tf_op jit(solution)/shard_map/ppermute | solution.py:34
  44.1 10.8 %all_gather.11 = bf16[256,1024]{1,0:T(8,128)(2,1)} all-gather(bf16[256,128]{1,0:T(8,128)(2,1)S(1)} %copy-done.6), channel_id=1, replica_groups=mesh['dp'=8,'tensor'=4] {'dp'}, dimensions={1}, use_global_device_ids=true | all-gather | bytes 589824 | tf_op jit(solution)/shard_map/all_gather | solution.py:41
  54.9 3.7 %collective-permute-done.2 = bf16[256,1024]{1,0:T(8,128)(2,1)S(1)} collective-permute-done((bf16[256,1024]{1,0:T(8,128)(2,1)S(1)}, bf16[256,1024]{1,0:T(8,128)(2,1)S(1)}, u32[]{:S(2)}, u32[]{:S(2)}) %collective-permute-start.2) | collective-permute-done | bytes 524320 | tf_op jit(solution)/shard_map/ppermute | solution.py:34
  65.8 3.8 %fusion.14 = bf16[1024,768]{1,0:T(8,128)(2,1)S(1)} fusion(bf16[1024,768]{1,0:T(8,128)(2,1)} %all-gather.3.cloned.1.call-done, bf16[2048,1024]{1,0:T(8,128)(2,1)} %constant_dynamic-update-slice_fusion, s32[]{:T(128)S(6)} %select_n.22), kind=kOutput, calls=%fused_computation.18 | convolution fusion | flops 1611399168 | bytes 5242884 | tf_op jit(solution)/shard_map/dot_general | solution.py:49
  69.7 5.2 %reshape.105 = bf16[16,64,4,3,64]{4,3,2,1,0:T(4,128)(2,1)} reshape(bf16[1024,768]{1,0:T(8,128)(2,1)S(1)} %fusion.14) | data formatting | bytes 3145728 | tf_op jit(solution)/shard_map/reshape | solution.py:52
  74.8 11.3 %fusion.83 = (bf16[16,64,4,1,64]{4,3,2,1,0:T(2,128)(2,1)S(1)}, bf16[16,64,4,1,64]{4,3,2,1,0:T(2,128)(2,1)}, bf16[16,64,4,1,64]{4,3,2,1,0:T(2,128)(2,1)}) fusion(bf16[16,64,4,3,64]{4,3,2,1,0:T(4,128)(2,1)} %reshape.105), kind=kLoop, calls=%fused_computation.92 | loop fusion | bytes 3145728 | tf_op jit(solution)/shard_map/slice | solution.py:55
  86.2 4.7 %fusion.84 = (f32[16,4,64]{2,1,0:T(4,128)S(1)}, f32[16,4,64,64]{2,3,1,0:T(8,128)}) fusion(pred[16,64]{1,0:T(8,128)(4,1)S(1)} %get-tuple-element.14, bf16[16,64,4,1,64]{4,3,2,1,0:T(2,128)(2,1)} %get-tuple-element.13, bf16[16,64,4,1,64]{4,3,2,1,0:T(2,128)(2,1)} %get-tuple-element.12), kind=kOutput, calls=%fused_computation.93 | convolution fusion | flops 34603072 | bytes 2114560 | tf_op jit(solution)/shard_map/sub | solution.py:62
  96.6 3.2 %fusion.43 = bf16[1024,256]{1,0:T(8,128)(2,1)} fusion(bf16[256,1024]{1,0:T(8,128)(2,1)} %all_gather.11, bf16[1024,1024]{1,0:T(8,128)(2,1)} %all-gather.5.cloned.1.call-done, bf16[1024]{0:T(1024)(128)(2,1)S(1)} %reshape.102), kind=kOutput, calls=%fused_computation.38 | convolution fusion | flops 538181632 | bytes 3147776 | tf_op jit(solution)/shard_map/dot_general | solution.py:74
  99.9 2.8 reshape.98
  104.9 3.1 %fusion.72 = f32[16,4,64,64]{2,3,1,0:T(8,128)} fusion(bf16[16,64,4,64]{1,3,2,0:T(8,128)(2,1)} %copy.48, bf16[16,64,4,1,64]{4,3,2,1,0:T(2,128)(2,1)S(1)} %get-tuple-element.11), kind=kOutput, calls=%fused_computation.67 | convolution fusion | flops 33554432 | bytes 2097152 | tf_op jit(solution)/shard_map/bqhe,bkhe->bhqk/dot_general | solution.py:78
  109.7 5.5 %fusion.40 = bf16[16,64,4,1,64]{1,4,2,0,3:T(8,128)(2,1)} fusion(f32[16,4,64,64]{2,3,1,0:T(8,128)} %fusion.72, bf16[16,64,4,1,64]{4,3,2,1,0:T(2,128)(2,1)S(1)} %copy-done.4, f32[16,4,64,64]{2,3,1,0:T(8,128)} %get-tuple-element.17, f32[16,4,64]{2,1,0:T(4,128)S(1)} %get-tuple-element.16), kind=kOutput, calls=%fused_computation.35 | convolution fusion | flops 35655744 | bytes 3162112 | tf_op jit(solution)/shard_map/bhqk,bkhe->bqhe/dot_general | solution.py:86
  115.2 3.3 %fusion.46 = bf16[256,1024]{1,0:T(8,128)(2,1)} fusion(bf16[1024,256]{0,1:T(8,128)(2,1)S(1)} %reshape.100, bf16[1024,1024]{1,0:T(8,128)(2,1)} %all-gather.5.cloned.1.call-done, bf16[1024]{0:T(1024)(128)(2,1)S(1)} %reshape.102), kind=kOutput, calls=%fused_computation.39 | convolution fusion | flops 538181632 | bytes 3147776 | tf_op jit(solution)/shard_map/dot_general | solution.py:68
  120.9 5.5 %fusion.37 = bf16[16,64,4,1,64]{1,4,2,0,3:T(8,128)(2,1)} fusion(f32[16,4,64,64]{2,3,1,0:T(8,128)} %fusion.72, bf16[16,64,4,1,64]{4,3,2,1,0:T(2,128)(2,1)S(1)} %copy-done.3, f32[16,4,64,64]{2,3,1,0:T(8,128)} %get-tuple-element.17, f32[16,4,64]{2,1,0:T(4,128)S(1)} %get-tuple-element.16), kind=kOutput, calls=%fused_computation.34 | convolution fusion | flops 35655744 | bytes 3162112 | tf_op jit(solution)/shard_map/bhqk,bqhe->bkhe/dot_general | solution.py:89
  126.5 2.7 pad_maximum_fusion
  129.1 4.2 %copy.50 = bf16[16,64,4,3,64]{1,0,4,3,2:T(8,128)(2,1)} copy(bf16[16,64,4,3,64]{1,4,2,0,3:T(8,128)(2,1)S(1)} %pad_maximum_fusion) | data formatting | bytes 3145728 | tf_op jit(solution)/shard_map/stack | solution.py:92
  133.3 4.5 %reshape.99 = bf16[1024,768]{0,1:T(8,128)(2,1)S(1)} reshape(bf16[16,64,4,3,64]{1,0,4,3,2:T(8,128)(2,1)} %copy.50) | data formatting | bytes 3145728 | tf_op jit(solution)/shard_map/reshape | solution.py:92
  137.8 4.6 %fusion.17 = bf16[1024,768]{1,0:T(8,128)(2,1)} fusion(bf16[1024,768]{0,1:T(8,128)(2,1)S(1)} %reshape.99, bf16[2048,1024]{1,0:T(8,128)(2,1)} %constant_dynamic-update-slice_fusion, s32[]{:T(128)S(6)} %select_n.22), kind=kOutput, calls=%fused_computation.19 | convolution fusion | flops 1611399168 | bytes 5242884 | tf_op jit(solution)/shard_map/dot_general | solution.py:95
  142.5 4.6 %convolution_convert_fusion = bf16[1024,1024]{1,0:T(8,128)(2,1)} fusion(bf16[1024,768]{0,1:T(8,128)(2,1)S(1)} %reshape.99, bf16[1024,768]{1,0:T(8,128)(2,1)} %all-gather.3.cloned.1.call-done), kind=kOutput, calls=%fused_computation.8 | convolution fusion | flops 1611661312 | bytes 5242880 | tf_op jit(solution)/shard_map/dot_general | solution.py:102
  147.3 4.8 %reduce-scatter.10.cloned.1.call-done = bf16[128,256]{1,0:T(8,128)(2,1)} async-done(((bf16[1024,256]{1,0:T(8,128)(2,1)}), bf16[128,256]{1,0:T(8,128)(2,1)}) %reduce-scatter.10.cloned.1.call-update) | async-done | bytes 65552
  153.7 39.9 %reduce-scatter.8.cloned.1.call-done = bf16[128,768]{1,0:T(8,128)(2,1)} async-done(((bf16[1024,768]{1,0:T(8,128)(2,1)}), bf16[128,768]{1,0:T(8,128)(2,1)}) %reduce-scatter.8.cloned.1.call-update) | async-done | bytes 196624 | tf_op jit(solution)/shard_map/reduce_scatter | solution.py:98
  195.3 44.1 %reduce-scatter.6.cloned.1.call-done = bf16[256,1024]{1,0:T(8,128)(2,1)} async-done(((bf16[1024,1024]{1,0:T(8,128)(2,1)}), bf16[256,1024]{1,0:T(8,128)(2,1)}) %reduce-scatter.6.cloned.1.call-update) | async-done | bytes 524304 | tf_op jit(solution)/shard_map/reduce_scatter | solution.py:101
  241.0 39.5 %all-reduce = (f32[1024]{0:T(1024)}, f32[1024]{0:T(1024)}) all-reduce(f32[1024]{0:T(1024)S(1)} %get-tuple-element.5, f32[1024]{0:T(1024)S(1)} %get-tuple-element.8), channel_id=1, replica_groups=mesh['dp'=8,'tensor'=4] {'dp','tensor'}, use_global_device_ids=true, to_apply=%region_11.12 | all-reduce | flops 2048 | bytes 16384 | tf_op jit(solution)/shard_map/psum | solution.py:109
  (64 shorter events, 31.7 us)
Async XLA Ops:
  7.2 36.7 %copy-start.8 = (s32[16]{0:T(128)S(1)}, s32[16]{0:T(128)}, u32[]{:S(2)}) copy-start(s32[16]{0:T(128)} %param.9) | copy-start | bytes 196
  7.2 36.9 %copy-start.6 = (bf16[256,128]{1,0:T(8,128)(2,1)S(1)}, bf16[256,128]{1,0:T(8,128)(2,1)}, u32[]{:S(2)}) copy-start(bf16[256,128]{1,0:T(8,128)(2,1)} %param.13) | copy-start | bytes 196612
  7.2 58.6 %all-gather.3.cloned.1.call-start = ((), (), s32[]{:S(2)}) async-start(), calls=%async_computation.3 | async-start | bytes 1769472 | tf_op jit(solution)/shard_map/all_gather | solution.py:40
  7.9 88.7 %all-gather.5.cloned.1.call-start = ((), (), s32[]{:S(2)}) async-start(), calls=%async_computation.4 | async-start | bytes 2621440 | tf_op jit(solution)/shard_map/all_gather | solution.py:42
  11.8 49.3 %copy-start = (bf16[256,1024]{1,0:T(8,128)(2,1)S(1)}, bf16[256,1024]{1,0:T(8,128)(2,1)}, u32[]{:S(2)}) copy-start(bf16[256,1024]{1,0:T(8,128)(2,1)} %param.7) | copy-start | bytes 1572868
  11.9 49.3 %copy-start.5 = (f32[1024]{0:T(1024)S(1)}, f32[1024]{0:T(1024)}, u32[]{:S(2)}) copy-start(f32[1024]{0:T(1024)} %param.10) | copy-start | bytes 12292
  11.9 49.3 %copy-start.7 = (f32[1024]{0:T(1024)S(1)}, f32[1024]{0:T(1024)}, u32[]{:S(2)}) copy-start(f32[1024]{0:T(1024)} %param.11) | copy-start | bytes 12292
  11.9 17.1 %collective-permute-start = (bf16[256,1024]{1,0:T(8,128)(2,1)S(1)}, bf16[256,1024]{1,0:T(8,128)(2,1)S(1)}, u32[]{:S(2)}, u32[]{:S(2)}) collective-permute-start(bf16[256,1024]{1,0:T(8,128)(2,1)S(1)} %fusion.54), channel_id=1, source_target_pairs={{0,1},{1,2},{2,3},{3,0},{4,5},{5,6},{6,7},{7,4},{8,9},{9,10},{10,1... | collective-permute-start | bytes 1572872 | tf_op jit(solution)/shard_map/ppermute | solution.py:34
  28.9 14.9 %collective-permute-start.1 = (bf16[256,1024]{1,0:T(8,128)(2,1)S(1)}, bf16[256,1024]{1,0:T(8,128)(2,1)S(1)}, u32[]{:S(2)}, u32[]{:S(2)}) collective-permute-start(bf16[256,1024]{1,0:T(8,128)(2,1)S(1)} %collective-permute-done), channel_id=1, source_target_pairs={{0,1},{1,2},{2,3},{3,0},{4,5},{5,6},{6,7},{7,4},{8,9},{9,10},{10,1... | collective-permute-start | bytes 1572872 | tf_op jit(solution)/shard_map/ppermute | solution.py:34
  43.8 14.8 %collective-permute-start.2 = (bf16[256,1024]{1,0:T(8,128)(2,1)S(1)}, bf16[256,1024]{1,0:T(8,128)(2,1)S(1)}, u32[]{:S(2)}, u32[]{:S(2)}) collective-permute-start(bf16[256,1024]{1,0:T(8,128)(2,1)S(1)} %collective-permute-done.1), channel_id=1, source_target_pairs={{0,1},{1,2},{2,3},{3,0},{4,5},{5,6},{6,7},{7,4},{8,9},{9,10},{10,1... | collective-permute-start | bytes 1572872 | tf_op jit(solution)/shard_map/ppermute | solution.py:34
  43.8 108.3 %reduce-scatter.10.cloned.1.call-start = ((), (), s32[]{:S(2)}) async-start(), calls=%async_computation.7 | async-start | bytes 589824
  104.9 3.1 %copy-start.1 = (bf16[16,64,4,64]{1,3,2,0:T(8,128)(2,1)S(1)}, bf16[16,64,4,64]{1,3,2,0:T(8,128)(2,1)}, u32[]{:S(2)}) copy-start(bf16[16,64,4,64]{1,3,2,0:T(8,128)(2,1)} %copy.48) | copy-start | bytes 1572868
  104.9 3.1 %copy-start.9 = (f32[16,4,64,64]{2,3,1,0:T(8,128)S(1)}, f32[16,4,64,64]{2,3,1,0:T(8,128)}, u32[]{:S(2)}) copy-start(f32[16,4,64,64]{2,3,1,0:T(8,128)} %get-tuple-element.17) | copy-start | bytes 3145732
  108.0 1.7 copy-start.4
  115.2 5.7 %copy-start.3 = (bf16[16,64,4,1,64]{4,3,2,1,0:T(2,128)(2,1)S(1)}, bf16[16,64,4,1,64]{4,3,2,1,0:T(2,128)(2,1)}, u32[]{:S(2)}) copy-start(bf16[16,64,4,1,64]{4,3,2,1,0:T(2,128)(2,1)} %get-tuple-element.12) | copy-start | bytes 1572868
  120.7 73.0 %reduce-scatter.8.cloned.1.call-start = ((), (), s32[]{:S(2)}) async-start(), calls=%async_computation.6 | async-start | bytes 1769472 | tf_op jit(solution)/shard_map/reduce_scatter | solution.py:98
  142.4 97.0 %reduce-scatter.6.cloned.1.call-start = ((), (), s32[]{:S(2)}) async-start(), calls=%async_computation.5 | async-start | bytes 2621440 | tf_op jit(solution)/shard_map/reduce_scatter | solution.py:101
  147.1 133.5 %copy-start.2 = (bf16[256,1024]{1,0:T(8,128)(2,1)S(1)}, bf16[256,1024]{1,0:T(8,128)(2,1)}, u32[]{:S(2)}) copy-start(bf16[256,1024]{1,0:T(8,128)(2,1)} %param.8) | copy-start | bytes 1572868
Sparse Core Ops, SparseCore 0:
  9.9 28.2 all-gather.2
  44.0 48.4 all-gather.4
  120.8 31.2 reduce-scatter.9
  155.3 38.3 reduce-scatter.7
  195.8 43.6 reduce-scatter.5
